TPU v7x, 32 devices: a whole 2x2x4 slice. The times are simulated.
32 devices in a mesh: gz: 8 (over z, x), gy: 4 (over y, core).
Axes of the slice: x: 2, y: 2, z: 4, core: 2. Of those that a mesh axis runs over, the one named last changes fastest.
Arguments:
- source_first: float32 [64, 32, 16, 128], P('gz', 'gy'), may hold values from -6 to 6
- source_second: float32 [32, 16, 16, 128], P('gz', 'gy'), may hold values from -6 to 6
- source_third: float32 [16, 8, 16, 128], P('gz', 'gy'), may hold values from -6 to 6
- source_fourth: float32 [8, 4, 16, 128], P('gz', 'gy'), may hold values from -6 to 6
- guess_first: float32 [64, 32, 16, 128], P('gz', 'gy'), may hold values from -6 to 6
- guess_second: float32 [32, 16, 16, 128], P('gz', 'gy'), may hold values from -6 to 6
- guess_third: float32 [16, 8, 16, 128], P('gz', 'gy'), may hold values from -6 to 6
- guess_fourth: float32 [8, 4, 16, 128], P('gz', 'gy'), may hold values from -6 to 6
- shift_first: float32 [64, 32, 128], P('gz', 'gy'), may hold values from 0.2 to 2
- shift_second: float32 [32, 16, 128], P('gz', 'gy'), may hold values from 0.2 to 2
- shift_third: float32 [16, 8, 128], P('gz', 'gy'), may hold values from 0.2 to 2
- shift_fourth: float32 [8, 4, 128], P('gz', 'gy'), may hold values from 0.2 to 2
- blocks_first: bfloat16 [64, 32, 2, 128, 128], P('gz', 'gy'), may hold values from -0.375 to 0.375
- blocks_second: bfloat16 [32, 16, 2, 128, 128], P('gz', 'gy'), may hold values from -0.375 to 0.375
- blocks_third: bfloat16 [16, 8, 2, 128, 128], P('gz', 'gy'), may hold values from -0.375 to 0.375
- links_first: int32 [64, 32, 2], P('gz', 'gy'), may hold values from 0 to 511, as said below
- links_second: int32 [32, 16, 2], P('gz', 'gy'), may hold values from 0 to 127, as said below
- links_third: int32 [16, 8, 2], P('gz', 'gy'), may hold values from 0 to 31, as said below
Outputs:
- smooth_first: float32 [64, 32, 16, 128], P('gz', 'gy')
- smooth_second: float32 [32, 16, 16, 128], P('gz', 'gy')
- smooth_third: float32 [16, 8, 16, 128], P('gz', 'gy')
- smooth_fourth: float32 [8, 4, 16, 128], P('gz', 'gy')
Inputs may be any that keep to these rules, and one draw needn't show every extreme that they name: `links_first`: entry k of fine cell (i, j) names coarse column x * 16 + y with x within one of i // 2 and y within one of j // 2, both periodic on the coarse grid. `links_second`: entry k of cell (i, j) names coarse column x * 8 + y with x within one of i // 2 and y within one of j // 2, both periodic on the coarse grid. `links_third`: entry k of cell (i, j) names coarse column x * 4 + y with x within one of i // 2 and y within one of j // 2, both periodic on the coarse grid.
All inputs are finite; a program needn't handle non-finite values.
Results may differ from a plain program's by a relative error of at most 0.0005.
Values may be sent and summed in bfloat16 or wider, within the bound.
A program may use at most 256 MiB of HBM per device.

v0:
```python
from functools import partial
import jax
import jax.numpy as jnp
from jax import lax
from jax.sharding import PartitionSpec as P

DEGREE = 3
upper_edge = 14.0
lower_edge = upper_edge / 8.0


def padded(x, sides, width):
    for axis, dim in sides:
        peers, length = (lax.axis_size(axis), x.shape[dim])
        up = [(i, (i + 1) % peers) for i in range(peers)]
        down = [(j, i) for i, j in up]
        last = lax.slice_in_dim(x, length - width, length, axis=dim)
        initial = lax.slice_in_dim(x, 0, width, axis=dim)
        before = lax.ppermute(last, axis, up)
        after = lax.ppermute(initial, axis, down)
        x = jnp.concatenate([before, x, after], axis=dim)
    return x


def chebyshev(source, initial, operator):
    centre = (upper_edge + lower_edge) / 2.0
    half_width = (upper_edge - lower_edge) / 2.0
    ratio_edge = centre / half_width
    factor = 1.0 / ratio_edge
    residual = source - operator(initial)
    direction = residual / centre
    result = initial
    for sweep_index in range(DEGREE):
        result = result + direction
        if sweep_index + 1 < DEGREE:
            residual = residual - operator(direction)
            factor_next = 1.0 / (2.0 * ratio_edge - factor)
            direction = factor_next * factor * direction + 2.0 * factor_next / half_width * residual
            factor = factor_next
    return result


def line_sum(vector):
    return jnp.roll(vector, 1, 3) + jnp.roll(vector, -1, 3)


def spread_apply(vector, diagonal):
    extended = padded(vector, (("gz", 0), ("gy", 1)), 1)
    beside = extended[2:, 1:-1] + extended[:-2, 1:-1] + extended[1:-1, 2:] + extended[1:-1, :-2]
    beside = beside + line_sum(vector)
    return (6.0 + diagonal[:, :, None, :]) * vector - beside


def slab_apply(vector, diagonal):
    extended = padded(vector, (("gz", 0),), 1)
    beside = extended[2:] + extended[:-2] + jnp.roll(vector, 1, 1) + jnp.roll(vector, -1, 1)
    beside = beside + line_sum(vector)
    return (6.0 + diagonal[:, :, None, :]) * vector - beside


def pack_level(source, initial, diagonal):
    return jnp.concatenate([source, initial, diagonal[:, :, None, :]], axis=2)


def level_smooth(source, initial, diagonal):
    return chebyshev(source, initial, partial(spread_apply, diagonal=diagonal))


def gathered_smooth(source, initial, diagonal):
    copies = source.shape[2]
    gathered = lax.all_gather(pack_level(source, initial, diagonal), "gy", axis=1, tiled=True)
    return chebyshev(
        gathered[:, :, :copies],
        gathered[:, :, copies : 2 * copies],
        partial(slab_apply, diagonal=gathered[:, :, 2 * copies]),
    )


def own_rows(gathered):
    row_count = gathered.shape[1] // lax.axis_size("gy")
    return lax.dynamic_slice_in_dim(gathered, lax.axis_index("gy") * row_count, row_count, 1)


def prolong_local(extended, link_ids, blocks, anchor_row, anchor_col, full_rows, full_cols):
    coarse_row = link_ids // full_cols
    coarse_col = link_ids % full_cols
    local_row = (coarse_row - anchor_row + 1) % full_rows
    local_col = (coarse_col - anchor_col + 1) % full_cols
    flat_index = local_row * extended.shape[1] + local_col
    picked_lines = extended.reshape((-1,) + extended.shape[2:])[flat_index]
    return jnp.einsum("abkrj,abkij->abri", picked_lines, blocks, preferred_element_type=jnp.float32)


def spread_prolong(coarse, link_ids, blocks):
    narrow = coarse.astype(jnp.bfloat16)
    extended = padded(narrow, (("gz", 0), ("gy", 1)), 1)
    return prolong_local(
        extended,
        link_ids,
        blocks,
        lax.axis_index("gz") * coarse.shape[0],
        lax.axis_index("gy") * coarse.shape[1],
        coarse.shape[0] * lax.axis_size("gz"),
        coarse.shape[1] * lax.axis_size("gy"),
    )


def slab_prolong(gathered, link_ids, blocks):
    narrow = gathered.astype(jnp.bfloat16)
    extended = padded(narrow, (("gz", 0),), 1)
    extended = jnp.concatenate([extended[:, -1:], extended, extended[:, :1]], axis=1)
    return prolong_local(
        extended,
        link_ids,
        blocks,
        lax.axis_index("gz") * gathered.shape[0],
        0,
        gathered.shape[0] * lax.axis_size("gz"),
        gathered.shape[1],
    )


def shards(
    source_first,
    source_second,
    source_third,
    source_fourth,
    guess_first,
    guess_second,
    guess_third,
    guess_fourth,
    shift_first,
    shift_second,
    shift_third,
    shift_fourth,
    blocks_first,
    blocks_second,
    blocks_third,
    links_first,
    links_second,
    links_third,
):
    fourth_whole = gathered_smooth(source_fourth, guess_fourth, shift_fourth)
    smooth_fourth = own_rows(fourth_whole)
    start_third = guess_third + slab_prolong(fourth_whole, links_third, blocks_third)
    third_whole = gathered_smooth(source_third, start_third, shift_third)
    smooth_third = own_rows(third_whole)
    start_second = guess_second + slab_prolong(third_whole, links_second, blocks_second)
    smooth_second = level_smooth(source_second, start_second, shift_second)
    start_first = guess_first + spread_prolong(smooth_second, links_first, blocks_first)
    smooth_first = level_smooth(source_first, start_first, shift_first)
    return (smooth_first, smooth_second, smooth_third, smooth_fourth)


def solution(mesh):
    in_specs = (
        P("gz", "gy", None, None),
        P("gz", "gy", None, None),
        P("gz", "gy", None, None),
        P("gz", "gy", None, None),
        P("gz", "gy", None, None),
        P("gz", "gy", None, None),
        P("gz", "gy", None, None),
        P("gz", "gy", None, None),
        P("gz", "gy", None),
        P("gz", "gy", None),
        P("gz", "gy", None),
        P("gz", "gy", None),
        P("gz", "gy", None, None, None),
        P("gz", "gy", None, None, None),
        P("gz", "gy", None, None, None),
        P("gz", "gy", None),
        P("gz", "gy", None),
        P("gz", "gy", None),
    )
    out_specs = (
        P("gz", "gy", None, None),
        P("gz", "gy", None, None),
        P("gz", "gy", None, None),
        P("gz", "gy", None, None),
    )
    return jax.shard_map(shards, mesh=mesh, in_specs=in_specs, out_specs=out_specs, check_vma=False)
```

profile of v0, /device:TPU:0, one launch (start us, length us, event | category | flops | bytes accessed | tf_op | source)
XLA Modules:
  0.0 166.0 jit_solution(16387655743293812934)
XLA Ops:
  1.5 6.2 %all_gather.6 = f32[1,4,33,128]{3,0,2,1:T(1,128)S(1)} all-gather(f32[1,1,33,128]{3,0,2,1:T(1,128)S(1)} %pad_maximum_fusion.85), channel_id=1, replica_groups=mesh['gz'=8,'gy'=4] {'gy'}, dimensions={1}, use_global_device_ids=true | all-gather | bytes 84480 | tf_op jit(solution)/shard_map/all_gather | solution.py:71
  7.7 2.0 %collective-permute-start.1 = (f32[1,4,16,128]{3,2,1,0:T(8,128)S(1)}, f32[1,4,16,128]{3,2,1,0:T(8,128)S(1)}, u32[]{:S(2)}, u32[]{:S(2)}) collective-permute-start(f32[1,4,16,128]{3,2,1,0:T(8,128)S(1)} %bitcast.49), channel_id=1, source_target_pairs={{0,4},{4,8},{8,12},{12,16},{16,20},{20,24},{24,28},{28,0},{1,5},{5... | collective-permute-start | bytes 98312 | tf_op jit(solution)/shard_map/ppermute | solution.py:19
  9.7 3.1 %collective-permute-start = (f32[1,4,16,128]{3,2,1,0:T(8,128)S(1)}, f32[1,4,16,128]{3,2,1,0:T(8,128)S(1)}, u32[]{:S(2)}, u32[]{:S(2)}) collective-permute-start(f32[1,4,16,128]{3,2,1,0:T(8,128)S(1)} %bitcast.50), channel_id=1, source_target_pairs={{4,0},{8,4},{12,8},{16,12},{20,16},{24,20},{28,24},{0,28},{5,1},{9... | collective-permute-start | bytes 98312 | tf_op jit(solution)/shard_map/ppermute | solution.py:20
  17.3 4.7 %collective-permute-start.2 = (f32[1,4,16,128]{3,2,1,0:T(8,128)S(1)}, f32[1,4,16,128]{3,2,1,0:T(8,128)S(1)}, u32[]{:S(2)}, u32[]{:S(2)}) collective-permute-start(f32[1,4,16,128]{3,2,1,0:T(8,128)S(1)} %get-tuple-element.28), channel_id=1, source_target_pairs={{4,0},{8,4},{12,8},{16,12},{20,16},{24,20},{28,24},{0,28},{5,1},{9... | collective-permute-start | bytes 98312 | tf_op jit(solution)/shard_map/ppermute | solution.py:20
  24.0 4.8 %collective-permute-start.4 = (f32[1,4,16,128]{3,2,1,0:T(8,128)S(1)}, f32[1,4,16,128]{3,2,1,0:T(8,128)S(1)}, u32[]{:S(2)}, u32[]{:S(2)}) collective-permute-start(f32[1,4,16,128]{3,2,1,0:T(8,128)S(1)} %get-tuple-element.26), channel_id=1, source_target_pairs={{4,0},{8,4},{12,8},{16,12},{20,16},{24,20},{28,24},{0,28},{5,1},{9... | collective-permute-start | bytes 98312 | tf_op jit(solution)/shard_map/ppermute | solution.py:20
  30.8 4.8 %collective-permute-start.7 = (bf16[1,4,16,128]{3,2,1,0:T(8,128)(2,1)S(1)}, bf16[1,4,16,128]{3,2,1,0:T(8,128)(2,1)S(1)}, u32[]{:S(2)}, u32[]{:S(2)}) collective-permute-start(bf16[1,4,16,128]{3,2,1,0:T(8,128)(2,1)S(1)} %get-tuple-element.24), channel_id=1, source_target_pairs={{4,0},{8,4},{12,8},{16,12},{20,16},{24,20},{28,24},{0,28},{5,1},{9... | collective-permute-start | bytes 49160 | tf_op jit(solution)/shard_map/ppermute | solution.py:20
  37.0 5.0 %collective-permute-done.6 = bf16[1,4,16,128]{3,2,1,0:T(8,128)(2,1)S(1)} collective-permute-done((bf16[1,4,16,128]{3,2,1,0:T(8,128)(2,1)S(1)}, bf16[1,4,16,128]{3,2,1,0:T(8,128)(2,1)S(1)}, u32[]{:S(2)}, u32[]{:S(2)}) %collective-permute-start.6) | collective-permute-done | bytes 16416 | tf_op jit(solution)/shard_map/ppermute | solution.py:19
  44.5 6.3 %all_gather.7 = f32[2,8,33,128]{3,2,1,0:T(8,128)S(1)} all-gather(f32[2,2,33,128]{3,2,1,0:T(8,128)S(1)} %pad_maximum_fusion.68), channel_id=1, replica_groups=mesh['gz'=8,'gy'=4] {'gy'}, dimensions={1}, use_global_device_ids=true | all-gather | bytes 337920 | tf_op jit(solution)/shard_map/all_gather | solution.py:71
  51.1 2.0 %collective-permute-start.9 = (f32[1,8,16,128]{3,2,1,0:T(8,128)S(1)}, f32[1,8,16,128]{3,2,1,0:T(8,128)S(1)}, u32[]{:S(2)}, u32[]{:S(2)}) collective-permute-start(f32[1,8,16,128]{3,2,1,0:T(8,128)S(1)} %get-tuple-element.55), channel_id=1, source_target_pairs={{0,4},{4,8},{8,12},{12,16},{16,20},{20,24},{24,28},{28,0},{1,5},{5... | collective-permute-start | bytes 196616 | tf_op jit(solution)/shard_map/ppermute | solution.py:19
  53.1 2.3 %collective-permute-done.8 = f32[1,8,16,128]{3,2,1,0:T(8,128)S(1)} collective-permute-done((f32[1,8,16,128]{3,2,1,0:T(8,128)S(1)}, f32[1,8,16,128]{3,2,1,0:T(8,128)S(1)}, u32[]{:S(2)}, u32[]{:S(2)}) %collective-permute-start.8) | collective-permute-done | bytes 65568 | tf_op jit(solution)/shard_map/ppermute | solution.py:20
  55.4 2.8 %collective-permute-done.9 = f32[1,8,16,128]{3,2,1,0:T(8,128)S(1)} collective-permute-done((f32[1,8,16,128]{3,2,1,0:T(8,128)S(1)}, f32[1,8,16,128]{3,2,1,0:T(8,128)S(1)}, u32[]{:S(2)}, u32[]{:S(2)}) %collective-permute-start.9) | collective-permute-done | bytes 65568 | tf_op jit(solution)/shard_map/ppermute | solution.py:19
  60.7 2.2 %collective-permute-done.10 = f32[1,8,16,128]{3,2,1,0:T(8,128)S(1)} collective-permute-done((f32[1,8,16,128]{3,2,1,0:T(8,128)S(1)}, f32[1,8,16,128]{3,2,1,0:T(8,128)S(1)}, u32[]{:S(2)}, u32[]{:S(2)}) %collective-permute-start.10) | collective-permute-done | bytes 65568 | tf_op jit(solution)/shard_map/ppermute | solution.py:20
  62.9 2.9 %collective-permute-done.11 = f32[1,8,16,128]{3,2,1,0:T(8,128)S(1)} collective-permute-done((f32[1,8,16,128]{3,2,1,0:T(8,128)S(1)}, f32[1,8,16,128]{3,2,1,0:T(8,128)S(1)}, u32[]{:S(2)}, u32[]{:S(2)}) %collective-permute-start.11) | collective-permute-done | bytes 65568 | tf_op jit(solution)/shard_map/ppermute | solution.py:19
  66.3 2.0 %collective-permute-start.13 = (f32[1,8,16,128]{3,2,1,0:T(8,128)S(1)}, f32[1,8,16,128]{3,2,1,0:T(8,128)S(1)}, u32[]{:S(2)}, u32[]{:S(2)}) collective-permute-start(f32[1,8,16,128]{3,2,1,0:T(8,128)S(1)} %get-tuple-element.89), channel_id=1, source_target_pairs={{0,4},{4,8},{8,12},{12,16},{16,20},{20,24},{24,28},{28,0},{1,5},{5... | collective-permute-start | bytes 196616 | tf_op jit(solution)/shard_map/ppermute | solution.py:19
  68.3 2.9 %collective-permute-done.12 = f32[1,8,16,128]{3,2,1,0:T(8,128)S(1)} collective-permute-done((f32[1,8,16,128]{3,2,1,0:T(8,128)S(1)}, f32[1,8,16,128]{3,2,1,0:T(8,128)S(1)}, u32[]{:S(2)}, u32[]{:S(2)}) %collective-permute-start.12) | collective-permute-done | bytes 65568 | tf_op jit(solution)/shard_map/ppermute | solution.py:20
  71.3 2.1 %collective-permute-done.13 = f32[1,8,16,128]{3,2,1,0:T(8,128)S(1)} collective-permute-done((f32[1,8,16,128]{3,2,1,0:T(8,128)S(1)}, f32[1,8,16,128]{3,2,1,0:T(8,128)S(1)}, u32[]{:S(2)}, u32[]{:S(2)}) %collective-permute-start.13) | collective-permute-done | bytes 65568 | tf_op jit(solution)/shard_map/ppermute | solution.py:19
  73.6 4.7 %collective-permute-start.15 = (bf16[1,8,16,128]{3,2,1,0:T(8,128)(2,1)S(1)}, bf16[1,8,16,128]{3,2,1,0:T(8,128)(2,1)S(1)}, u32[]{:S(2)}, u32[]{:S(2)}) collective-permute-start(bf16[1,8,16,128]{3,2,1,0:T(8,128)(2,1)S(1)} %get-tuple-element.123), channel_id=1, source_target_pairs={{4,0},{8,4},{12,8},{16,12},{20,16},{24,20},{28,24},{0,28},{5,1},{9... | collective-permute-start | bytes 98312 | tf_op jit(solution)/shard_map/ppermute | solution.py:20
  81.3 4.9 %collective-permute-start.16 = (f32[1,4,16,128]{3,2,1,0:T(8,128)S(1)}, f32[1,4,16,128]{3,2,1,0:T(8,128)S(1)}, u32[]{:S(2)}, u32[]{:S(2)}) collective-permute-start(f32[1,4,16,128]{3,2,1,0:T(8,128)S(1)} %get-tuple-element.83), channel_id=1, source_target_pairs={{4,0},{8,4},{12,8},{16,12},{20,16},{24,20},{28,24},{0,28},{5,1},{9... | collective-permute-start | bytes 98312 | tf_op jit(solution)/shard_map/ppermute | solution.py:20
  89.8 2.2 %collective-permute-done.19 = f32[6,1,16,128]{3,2,1,0:T(8,128)S(1)} collective-permute-done((f32[6,1,16,128]{3,2,1,0:T(8,128)S(1)}, f32[6,1,16,128]{3,2,1,0:T(8,128)S(1)}, u32[]{:S(2)}, u32[]{:S(2)}) %collective-permute-start.19) | collective-permute-done | bytes 49184 | tf_op jit(solution)/shard_map/ppermute | solution.py:19
  92.2 4.8 %collective-permute-start.20 = (f32[1,4,16,128]{3,2,1,0:T(8,128)S(1)}, f32[1,4,16,128]{3,2,1,0:T(8,128)S(1)}, u32[]{:S(2)}, u32[]{:S(2)}) collective-permute-start(f32[1,4,16,128]{3,2,1,0:T(8,128)S(1)} %get-tuple-element.77), channel_id=1, source_target_pairs={{4,0},{8,4},{12,8},{16,12},{20,16},{24,20},{28,24},{0,28},{5,1},{9... | collective-permute-start | bytes 98312 | tf_op jit(solution)/shard_map/ppermute | solution.py:20
  102.8 4.8 %collective-permute-start.24 = (f32[1,4,16,128]{3,2,1,0:T(8,128)S(1)}, f32[1,4,16,128]{3,2,1,0:T(8,128)S(1)}, u32[]{:S(2)}, u32[]{:S(2)}) collective-permute-start(f32[1,4,16,128]{3,2,1,0:T(8,128)S(1)} %get-tuple-element.71), channel_id=1, source_target_pairs={{4,0},{8,4},{12,8},{16,12},{20,16},{24,20},{28,24},{0,28},{5,1},{9... | collective-permute-start | bytes 98312 | tf_op jit(solution)/shard_map/ppermute | solution.py:20
  114.0 4.8 %collective-permute-start.29 = (bf16[1,4,16,128]{3,2,1,0:T(8,128)(2,1)S(1)}, bf16[1,4,16,128]{3,2,1,0:T(8,128)(2,1)S(1)}, u32[]{:S(2)}, u32[]{:S(2)}) collective-permute-start(bf16[1,4,16,128]{3,2,1,0:T(8,128)(2,1)S(1)} %get-tuple-element.121), channel_id=1, source_target_pairs={{4,0},{8,4},{12,8},{16,12},{20,16},{24,20},{28,24},{0,28},{5,1},{9... | collective-permute-start | bytes 49160 | tf_op jit(solution)/shard_map/ppermute | solution.py:20
  124.5 3.4 %fusion = f32[8,8,16,128]{3,2,1,0:T(8,128)S(1)} fusion(f32[8,8,16,128]{3,2,1,0:T(8,128)S(1)} %copy-done.2, bf16[8,8,2,16,128]{4,3,2,1,0:T(8,128)(2,1)S(1)} %bitcast.46, bf16[8,8,2,128,128]{4,3,2,1,0:T(8,128)(2,1)} %param.30), kind=kOutput, calls=%fused_computation.4 | convolution fusion | flops 67239936 | bytes 5767168 | tf_op jit(solution)/shard_map/abkrj,abkij->abri/dot_general | solution.py:91
  128.1 4.8 %collective-permute-start.32 = (f32[1,8,16,128]{3,2,1,0:T(8,128)S(1)}, f32[1,8,16,128]{3,2,1,0:T(8,128)S(1)}, u32[]{:S(2)}, u32[]{:S(2)}) collective-permute-start(f32[1,8,16,128]{3,2,1,0:T(8,128)S(1)} %get-tuple-element.49), channel_id=1, source_target_pairs={{4,0},{8,4},{12,8},{16,12},{20,16},{24,20},{28,24},{0,28},{5,1},{9... | collective-permute-start | bytes 196616 | tf_op jit(solution)/shard_map/ppermute | solution.py:20
  133.0 2.3 %collective-permute-done.33 = f32[1,8,16,128]{3,2,1,0:T(8,128)S(1)} collective-permute-done((f32[1,8,16,128]{3,2,1,0:T(8,128)S(1)}, f32[1,8,16,128]{3,2,1,0:T(8,128)S(1)}, u32[]{:S(2)}, u32[]{:S(2)}) %collective-permute-start.33) | collective-permute-done | bytes 65568 | tf_op jit(solution)/shard_map/ppermute | solution.py:19
  136.4 2.2 %collective-permute-done.34 = f32[10,1,16,128]{3,2,1,0:T(8,128)S(1)} collective-permute-done((f32[10,1,16,128]{3,2,1,0:T(8,128)S(1)}, f32[10,1,16,128]{3,2,1,0:T(8,128)S(1)}, u32[]{:S(2)}, u32[]{:S(2)}) %collective-permute-start.34) | collective-permute-done | bytes 81952 | tf_op jit(solution)/shard_map/ppermute | solution.py:20
  138.6 2.0 %collective-permute-done.35 = f32[10,1,16,128]{3,2,1,0:T(8,128)S(1)} collective-permute-done((f32[10,1,16,128]{3,2,1,0:T(8,128)S(1)}, f32[10,1,16,128]{3,2,1,0:T(8,128)S(1)}, u32[]{:S(2)}, u32[]{:S(2)}) %collective-permute-start.35) | collective-permute-done | bytes 81952 | tf_op jit(solution)/shard_map/ppermute | solution.py:19
  141.1 5.0 %collective-permute-start.36 = (f32[1,8,16,128]{3,2,1,0:T(8,128)S(1)}, f32[1,8,16,128]{3,2,1,0:T(8,128)S(1)}, u32[]{:S(2)}, u32[]{:S(2)}) collective-permute-start(f32[1,8,16,128]{3,2,1,0:T(8,128)S(1)} %get-tuple-element.43), channel_id=1, source_target_pairs={{4,0},{8,4},{12,8},{16,12},{20,16},{24,20},{28,24},{0,28},{5,1},{9... | collective-permute-start | bytes 196616 | tf_op jit(solution)/shard_map/ppermute | solution.py:20
  146.3 2.0 %collective-permute-done.37 = f32[1,8,16,128]{3,2,1,0:T(8,128)S(1)} collective-permute-done((f32[1,8,16,128]{3,2,1,0:T(8,128)S(1)}, f32[1,8,16,128]{3,2,1,0:T(8,128)S(1)}, u32[]{:S(2)}, u32[]{:S(2)}) %collective-permute-start.37) | collective-permute-done | bytes 65568 | tf_op jit(solution)/shard_map/ppermute | solution.py:19
  153.2 4.8 %collective-permute-start.40 = (f32[1,8,16,128]{3,2,1,0:T(8,128)S(1)}, f32[1,8,16,128]{3,2,1,0:T(8,128)S(1)}, u32[]{:S(2)}, u32[]{:S(2)}) collective-permute-start(f32[1,8,16,128]{3,2,1,0:T(8,128)S(1)} %get-tuple-element.41), channel_id=1, source_target_pairs={{4,0},{8,4},{12,8},{16,12},{20,16},{24,20},{28,24},{0,28},{5,1},{9... | collective-permute-start | bytes 196616 | tf_op jit(solution)/shard_map/ppermute | solution.py:20
  158.2 2.0 %collective-permute-done.41 = f32[1,8,16,128]{3,2,1,0:T(8,128)S(1)} collective-permute-done((f32[1,8,16,128]{3,2,1,0:T(8,128)S(1)}, f32[1,8,16,128]{3,2,1,0:T(8,128)S(1)}, u32[]{:S(2)}, u32[]{:S(2)}) %collective-permute-start.41) | collective-permute-done | bytes 65568 | tf_op jit(solution)/shard_map/ppermute | solution.py:19
  162.5 2.1 %collective-permute-done.43 = f32[10,1,16,128]{3,2,1,0:T(8,128)S(1)} collective-permute-done((f32[10,1,16,128]{3,2,1,0:T(8,128)S(1)}, f32[10,1,16,128]{3,2,1,0:T(8,128)S(1)}, u32[]{:S(2)}, u32[]{:S(2)}) %collective-permute-start.43) | collective-permute-done | bytes 81952 | tf_op jit(solution)/shard_map/ppermute | solution.py:19
  (166 shorter events, 51.9 us)
Async XLA Ops:
  7.7 9.4 %collective-permute-start.1 = (f32[1,4,16,128]{3,2,1,0:T(8,128)S(1)}, f32[1,4,16,128]{3,2,1,0:T(8,128)S(1)}, u32[]{:S(2)}, u32[]{:S(2)}) collective-permute-start(f32[1,4,16,128]{3,2,1,0:T(8,128)S(1)} %bitcast.49), channel_id=1, source_target_pairs={{0,4},{4,8},{8,12},{12,16},{16,20},{20,24},{24,28},{28,0},{1,5},{5... | collective-permute-start | bytes 98312 | tf_op jit(solution)/shard_map/ppermute | solution.py:19
  9.7 7.4 %collective-permute-start = (f32[1,4,16,128]{3,2,1,0:T(8,128)S(1)}, f32[1,4,16,128]{3,2,1,0:T(8,128)S(1)}, u32[]{:S(2)}, u32[]{:S(2)}) collective-permute-start(f32[1,4,16,128]{3,2,1,0:T(8,128)S(1)} %bitcast.50), channel_id=1, source_target_pairs={{4,0},{8,4},{12,8},{16,12},{20,16},{24,20},{28,24},{0,28},{5,1},{9... | collective-permute-start | bytes 98312 | tf_op jit(solution)/shard_map/ppermute | solution.py:20
  17.2 6.7 %collective-permute-start.3 = (f32[1,4,16,128]{3,2,1,0:T(8,128)S(1)}, f32[1,4,16,128]{3,2,1,0:T(8,128)S(1)}, u32[]{:S(2)}, u32[]{:S(2)}) collective-permute-start(f32[1,4,16,128]{3,2,1,0:T(8,128)S(1)} %get-tuple-element.28), channel_id=1, source_target_pairs={{0,4},{4,8},{8,12},{12,16},{16,20},{20,24},{24,28},{28,0},{1,5},{5... | collective-permute-start | bytes 98312 | tf_op jit(solution)/shard_map/ppermute | solution.py:19
  17.3 6.6 %collective-permute-start.2 = (f32[1,4,16,128]{3,2,1,0:T(8,128)S(1)}, f32[1,4,16,128]{3,2,1,0:T(8,128)S(1)}, u32[]{:S(2)}, u32[]{:S(2)}) collective-permute-start(f32[1,4,16,128]{3,2,1,0:T(8,128)S(1)} %get-tuple-element.28), channel_id=1, source_target_pairs={{4,0},{8,4},{12,8},{16,12},{20,16},{24,20},{28,24},{0,28},{5,1},{9... | collective-permute-start | bytes 98312 | tf_op jit(solution)/shard_map/ppermute | solution.py:20
  24.0 6.7 %collective-permute-start.5 = (f32[1,4,16,128]{3,2,1,0:T(8,128)S(1)}, f32[1,4,16,128]{3,2,1,0:T(8,128)S(1)}, u32[]{:S(2)}, u32[]{:S(2)}) collective-permute-start(f32[1,4,16,128]{3,2,1,0:T(8,128)S(1)} %get-tuple-element.26), channel_id=1, source_target_pairs={{0,4},{4,8},{8,12},{12,16},{16,20},{20,24},{24,28},{28,0},{1,5},{5... | collective-permute-start | bytes 98312 | tf_op jit(solution)/shard_map/ppermute | solution.py:19
  24.0 6.6 %collective-permute-start.4 = (f32[1,4,16,128]{3,2,1,0:T(8,128)S(1)}, f32[1,4,16,128]{3,2,1,0:T(8,128)S(1)}, u32[]{:S(2)}, u32[]{:S(2)}) collective-permute-start(f32[1,4,16,128]{3,2,1,0:T(8,128)S(1)} %get-tuple-element.26), channel_id=1, source_target_pairs={{4,0},{8,4},{12,8},{16,12},{20,16},{24,20},{28,24},{0,28},{5,1},{9... | collective-permute-start | bytes 98312 | tf_op jit(solution)/shard_map/ppermute | solution.py:20
  30.8 6.3 %collective-permute-start.7 = (bf16[1,4,16,128]{3,2,1,0:T(8,128)(2,1)S(1)}, bf16[1,4,16,128]{3,2,1,0:T(8,128)(2,1)S(1)}, u32[]{:S(2)}, u32[]{:S(2)}) collective-permute-start(bf16[1,4,16,128]{3,2,1,0:T(8,128)(2,1)S(1)} %get-tuple-element.24), channel_id=1, source_target_pairs={{4,0},{8,4},{12,8},{16,12},{20,16},{24,20},{28,24},{0,28},{5,1},{9... | collective-permute-start | bytes 49160 | tf_op jit(solution)/shard_map/ppermute | solution.py:20
  35.6 6.4 %collective-permute-start.6 = (bf16[1,4,16,128]{3,2,1,0:T(8,128)(2,1)S(1)}, bf16[1,4,16,128]{3,2,1,0:T(8,128)(2,1)S(1)}, u32[]{:S(2)}, u32[]{:S(2)}) collective-permute-start(bf16[1,4,16,128]{3,2,1,0:T(8,128)(2,1)S(1)} %get-tuple-element.24), channel_id=1, source_target_pairs={{0,4},{4,8},{8,12},{12,16},{16,20},{20,24},{24,28},{28,0},{1,5},{5... | collective-permute-start | bytes 49160 | tf_op jit(solution)/shard_map/ppermute | solution.py:19
  51.0 4.4 %collective-permute-start.8 = (f32[1,8,16,128]{3,2,1,0:T(8,128)S(1)}, f32[1,8,16,128]{3,2,1,0:T(8,128)S(1)}, u32[]{:S(2)}, u32[]{:S(2)}) collective-permute-start(f32[1,8,16,128]{3,2,1,0:T(8,128)S(1)} %get-tuple-element.54), channel_id=1, source_target_pairs={{4,0},{8,4},{12,8},{16,12},{20,16},{24,20},{28,24},{0,28},{5,1},{9... | collective-permute-start | bytes 196616 | tf_op jit(solution)/shard_map/ppermute | solution.py:20
  51.1 7.1 %collective-permute-start.9 = (f32[1,8,16,128]{3,2,1,0:T(8,128)S(1)}, f32[1,8,16,128]{3,2,1,0:T(8,128)S(1)}, u32[]{:S(2)}, u32[]{:S(2)}) collective-permute-start(f32[1,8,16,128]{3,2,1,0:T(8,128)S(1)} %get-tuple-element.55), channel_id=1, source_target_pairs={{0,4},{4,8},{8,12},{12,16},{16,20},{20,24},{24,28},{28,0},{1,5},{5... | collective-permute-start | bytes 196616 | tf_op jit(solution)/shard_map/ppermute | solution.py:19
  58.6 4.3 %collective-permute-start.10 = (f32[1,8,16,128]{3,2,1,0:T(8,128)S(1)}, f32[1,8,16,128]{3,2,1,0:T(8,128)S(1)}, u32[]{:S(2)}, u32[]{:S(2)}) collective-permute-start(f32[1,8,16,128]{3,2,1,0:T(8,128)S(1)} %get-tuple-element.98), channel_id=1, source_target_pairs={{4,0},{8,4},{12,8},{16,12},{20,16},{24,20},{28,24},{0,28},{5,1},{9... | collective-permute-start | bytes 196616 | tf_op jit(solution)/shard_map/ppermute | solution.py:20
  58.9 7.0 %collective-permute-start.11 = (f32[1,8,16,128]{3,2,1,0:T(8,128)S(1)}, f32[1,8,16,128]{3,2,1,0:T(8,128)S(1)}, u32[]{:S(2)}, u32[]{:S(2)}) collective-permute-start(f32[1,8,16,128]{3,2,1,0:T(8,128)S(1)} %get-tuple-element.99), channel_id=1, source_target_pairs={{0,4},{4,8},{8,12},{12,16},{16,20},{20,24},{24,28},{28,0},{1,5},{5... | collective-permute-start | bytes 196616 | tf_op jit(solution)/shard_map/ppermute | solution.py:19
  66.2 5.0 %collective-permute-start.12 = (f32[1,8,16,128]{3,2,1,0:T(8,128)S(1)}, f32[1,8,16,128]{3,2,1,0:T(8,128)S(1)}, u32[]{:S(2)}, u32[]{:S(2)}) collective-permute-start(f32[1,8,16,128]{3,2,1,0:T(8,128)S(1)} %get-tuple-element.88), channel_id=1, source_target_pairs={{4,0},{8,4},{12,8},{16,12},{20,16},{24,20},{28,24},{0,28},{5,1},{9... | collective-permute-start | bytes 196616 | tf_op jit(solution)/shard_map/ppermute | solution.py:20
  66.3 7.0 %collective-permute-start.13 = (f32[1,8,16,128]{3,2,1,0:T(8,128)S(1)}, f32[1,8,16,128]{3,2,1,0:T(8,128)S(1)}, u32[]{:S(2)}, u32[]{:S(2)}) collective-permute-start(f32[1,8,16,128]{3,2,1,0:T(8,128)S(1)} %get-tuple-element.89), channel_id=1, source_target_pairs={{0,4},{4,8},{8,12},{12,16},{16,20},{20,24},{24,28},{28,0},{1,5},{5... | collective-permute-start | bytes 196616 | tf_op jit(solution)/shard_map/ppermute | solution.py:19
  73.5 6.7 %collective-permute-start.14 = (bf16[1,8,16,128]{3,2,1,0:T(8,128)(2,1)S(1)}, bf16[1,8,16,128]{3,2,1,0:T(8,128)(2,1)S(1)}, u32[]{:S(2)}, u32[]{:S(2)}) collective-permute-start(bf16[1,8,16,128]{3,2,1,0:T(8,128)(2,1)S(1)} %get-tuple-element.122), channel_id=1, source_target_pairs={{0,4},{4,8},{8,12},{12,16},{16,20},{20,24},{24,28},{28,0},{1,5},{5... | collective-permute-start | bytes 98312 | tf_op jit(solution)/shard_map/ppermute | solution.py:19
  73.6 6.6 %collective-permute-start.15 = (bf16[1,8,16,128]{3,2,1,0:T(8,128)(2,1)S(1)}, bf16[1,8,16,128]{3,2,1,0:T(8,128)(2,1)S(1)}, u32[]{:S(2)}, u32[]{:S(2)}) collective-permute-start(bf16[1,8,16,128]{3,2,1,0:T(8,128)(2,1)S(1)} %get-tuple-element.123), channel_id=1, source_target_pairs={{4,0},{8,4},{12,8},{16,12},{20,16},{24,20},{28,24},{0,28},{5,1},{9... | collective-permute-start | bytes 98312 | tf_op jit(solution)/shard_map/ppermute | solution.py:20
  81.2 6.8 %collective-permute-start.17 = (f32[1,4,16,128]{3,2,1,0:T(8,128)S(1)}, f32[1,4,16,128]{3,2,1,0:T(8,128)S(1)}, u32[]{:S(2)}, u32[]{:S(2)}) collective-permute-start(f32[1,4,16,128]{3,2,1,0:T(8,128)S(1)} %get-tuple-element.82), channel_id=1, source_target_pairs={{0,4},{4,8},{8,12},{12,16},{16,20},{20,24},{24,28},{28,0},{1,5},{5... | collective-permute-start | bytes 98312 | tf_op jit(solution)/shard_map/ppermute | solution.py:19
  81.3 6.7 %collective-permute-start.16 = (f32[1,4,16,128]{3,2,1,0:T(8,128)S(1)}, f32[1,4,16,128]{3,2,1,0:T(8,128)S(1)}, u32[]{:S(2)}, u32[]{:S(2)}) collective-permute-start(f32[1,4,16,128]{3,2,1,0:T(8,128)S(1)} %get-tuple-element.83), channel_id=1, source_target_pairs={{4,0},{8,4},{12,8},{16,12},{20,16},{24,20},{28,24},{0,28},{5,1},{9... | collective-permute-start | bytes 98312 | tf_op jit(solution)/shard_map/ppermute | solution.py:20
  92.2 6.7 %collective-permute-start.21 = (f32[1,4,16,128]{3,2,1,0:T(8,128)S(1)}, f32[1,4,16,128]{3,2,1,0:T(8,128)S(1)}, u32[]{:S(2)}, u32[]{:S(2)}) collective-permute-start(f32[1,4,16,128]{3,2,1,0:T(8,128)S(1)} %get-tuple-element.76), channel_id=1, source_target_pairs={{0,4},{4,8},{8,12},{12,16},{16,20},{20,24},{24,28},{28,0},{1,5},{5... | collective-permute-start | bytes 98312 | tf_op jit(solution)/shard_map/ppermute | solution.py:19
  92.2 6.7 %collective-permute-start.20 = (f32[1,4,16,128]{3,2,1,0:T(8,128)S(1)}, f32[1,4,16,128]{3,2,1,0:T(8,128)S(1)}, u32[]{:S(2)}, u32[]{:S(2)}) collective-permute-start(f32[1,4,16,128]{3,2,1,0:T(8,128)S(1)} %get-tuple-element.77), channel_id=1, source_target_pairs={{4,0},{8,4},{12,8},{16,12},{20,16},{24,20},{28,24},{0,28},{5,1},{9... | collective-permute-start | bytes 98312 | tf_op jit(solution)/shard_map/ppermute | solution.py:20
  102.7 6.7 %collective-permute-start.25 = (f32[1,4,16,128]{3,2,1,0:T(8,128)S(1)}, f32[1,4,16,128]{3,2,1,0:T(8,128)S(1)}, u32[]{:S(2)}, u32[]{:S(2)}) collective-permute-start(f32[1,4,16,128]{3,2,1,0:T(8,128)S(1)} %get-tuple-element.70), channel_id=1, source_target_pairs={{0,4},{4,8},{8,12},{12,16},{16,20},{20,24},{24,28},{28,0},{1,5},{5... | collective-permute-start | bytes 98312 | tf_op jit(solution)/shard_map/ppermute | solution.py:19
  102.8 6.7 %collective-permute-start.24 = (f32[1,4,16,128]{3,2,1,0:T(8,128)S(1)}, f32[1,4,16,128]{3,2,1,0:T(8,128)S(1)}, u32[]{:S(2)}, u32[]{:S(2)}) collective-permute-start(f32[1,4,16,128]{3,2,1,0:T(8,128)S(1)} %get-tuple-element.71), channel_id=1, source_target_pairs={{4,0},{8,4},{12,8},{16,12},{20,16},{24,20},{28,24},{0,28},{5,1},{9... | collective-permute-start | bytes 98312 | tf_op jit(solution)/shard_map/ppermute | solution.py:20
  114.0 6.5 %collective-permute-start.28 = (bf16[1,4,16,128]{3,2,1,0:T(8,128)(2,1)S(1)}, bf16[1,4,16,128]{3,2,1,0:T(8,128)(2,1)S(1)}, u32[]{:S(2)}, u32[]{:S(2)}) collective-permute-start(bf16[1,4,16,128]{3,2,1,0:T(8,128)(2,1)S(1)} %get-tuple-element.120), channel_id=1, source_target_pairs={{0,4},{4,8},{8,12},{12,16},{16,20},{20,24},{24,28},{28,0},{1,5},{5... | collective-permute-start | bytes 49160 | tf_op jit(solution)/shard_map/ppermute | solution.py:19
  114.0 6.5 %collective-permute-start.29 = (bf16[1,4,16,128]{3,2,1,0:T(8,128)(2,1)S(1)}, bf16[1,4,16,128]{3,2,1,0:T(8,128)(2,1)S(1)}, u32[]{:S(2)}, u32[]{:S(2)}) collective-permute-start(bf16[1,4,16,128]{3,2,1,0:T(8,128)(2,1)S(1)} %get-tuple-element.121), channel_id=1, source_target_pairs={{4,0},{8,4},{12,8},{16,12},{20,16},{24,20},{28,24},{0,28},{5,1},{9... | collective-permute-start | bytes 49160 | tf_op jit(solution)/shard_map/ppermute | solution.py:20
  128.0 7.3 %collective-permute-start.33 = (f32[1,8,16,128]{3,2,1,0:T(8,128)S(1)}, f32[1,8,16,128]{3,2,1,0:T(8,128)S(1)}, u32[]{:S(2)}, u32[]{:S(2)}) collective-permute-start(f32[1,8,16,128]{3,2,1,0:T(8,128)S(1)} %get-tuple-element.48), channel_id=1, source_target_pairs={{0,4},{4,8},{8,12},{12,16},{16,20},{20,24},{24,28},{28,0},{1,5},{5... | collective-permute-start | bytes 196616 | tf_op jit(solution)/shard_map/ppermute | solution.py:19
  128.1 7.3 %collective-permute-start.32 = (f32[1,8,16,128]{3,2,1,0:T(8,128)S(1)}, f32[1,8,16,128]{3,2,1,0:T(8,128)S(1)}, u32[]{:S(2)}, u32[]{:S(2)}) collective-permute-start(f32[1,8,16,128]{3,2,1,0:T(8,128)S(1)} %get-tuple-element.49), channel_id=1, source_target_pairs={{4,0},{8,4},{12,8},{16,12},{20,16},{24,20},{28,24},{0,28},{5,1},{9... | collective-permute-start | bytes 196616 | tf_op jit(solution)/shard_map/ppermute | solution.py:20
  136.2 4.3 %collective-permute-start.35 = (f32[10,1,16,128]{3,2,1,0:T(8,128)S(1)}, f32[10,1,16,128]{3,2,1,0:T(8,128)S(1)}, u32[]{:S(2)}, u32[]{:S(2)}) collective-permute-start(f32[10,1,16,128]{3,2,1,0:T(8,128)S(1)} %get-tuple-element.35), channel_id=1, source_target_pairs={{0,1},{1,2},{2,3},{3,0},{4,5},{5,6},{6,7},{7,4},{8,9},{9,10},{10,1... | collective-permute-start | bytes 245768 | tf_op jit(solution)/shard_map/ppermute | solution.py:19
  141.0 7.3 %collective-permute-start.37 = (f32[1,8,16,128]{3,2,1,0:T(8,128)S(1)}, f32[1,8,16,128]{3,2,1,0:T(8,128)S(1)}, u32[]{:S(2)}, u32[]{:S(2)}) collective-permute-start(f32[1,8,16,128]{3,2,1,0:T(8,128)S(1)} %get-tuple-element.42), channel_id=1, source_target_pairs={{0,4},{4,8},{8,12},{12,16},{16,20},{20,24},{24,28},{28,0},{1,5},{5... | collective-permute-start | bytes 196616 | tf_op jit(solution)/shard_map/ppermute | solution.py:19
  141.1 7.2 %collective-permute-start.36 = (f32[1,8,16,128]{3,2,1,0:T(8,128)S(1)}, f32[1,8,16,128]{3,2,1,0:T(8,128)S(1)}, u32[]{:S(2)}, u32[]{:S(2)}) collective-permute-start(f32[1,8,16,128]{3,2,1,0:T(8,128)S(1)} %get-tuple-element.43), channel_id=1, source_target_pairs={{4,0},{8,4},{12,8},{16,12},{20,16},{24,20},{28,24},{0,28},{5,1},{9... | collective-permute-start | bytes 196616 | tf_op jit(solution)/shard_map/ppermute | solution.py:20
  153.1 7.1 %collective-permute-start.41 = (f32[1,8,16,128]{3,2,1,0:T(8,128)S(1)}, f32[1,8,16,128]{3,2,1,0:T(8,128)S(1)}, u32[]{:S(2)}, u32[]{:S(2)}) collective-permute-start(f32[1,8,16,128]{3,2,1,0:T(8,128)S(1)} %get-tuple-element.40), channel_id=1, source_target_pairs={{0,4},{4,8},{8,12},{12,16},{16,20},{20,24},{24,28},{28,0},{1,5},{5... | collective-permute-start | bytes 196616 | tf_op jit(solution)/shard_map/ppermute | solution.py:19
  153.2 7.0 %collective-permute-start.40 = (f32[1,8,16,128]{3,2,1,0:T(8,128)S(1)}, f32[1,8,16,128]{3,2,1,0:T(8,128)S(1)}, u32[]{:S(2)}, u32[]{:S(2)}) collective-permute-start(f32[1,8,16,128]{3,2,1,0:T(8,128)S(1)} %get-tuple-element.41), channel_id=1, source_target_pairs={{4,0},{8,4},{12,8},{16,12},{20,16},{24,20},{28,24},{0,28},{5,1},{9... | collective-permute-start | bytes 196616 | tf_op jit(solution)/shard_map/ppermute | solution.py:20
  160.3 4.4 %collective-permute-start.43 = (f32[10,1,16,128]{3,2,1,0:T(8,128)S(1)}, f32[10,1,16,128]{3,2,1,0:T(8,128)S(1)}, u32[]{:S(2)}, u32[]{:S(2)}) collective-permute-start(f32[10,1,16,128]{3,2,1,0:T(8,128)S(1)} %get-tuple-element.31), channel_id=1, source_target_pairs={{0,1},{1,2},{2,3},{3,0},{4,5},{5,6},{6,7},{7,4},{8,9},{9,10},{10,1... | collective-permute-start | bytes 245768 | tf_op jit(solution)/shard_map/ppermute | solution.py:19
  (17 other events, 212.8 us)
where the time goes:
time: 166 us
  starting transfers between devices  70.2 us (42%)
  waiting for transfers between devices  60.8 us (37%)
  blocking collectives  12.5 us (8%)
  other arithmetic  9.63 us (6%)
  local copies, waits for them, and re-layouts  6.72 us (4%)
  matrix products  4.93 us (3%)
    ppermute x22, starting transfers between devices, padded(): after = lax.ppermute(initial, axis, down)  59.3 us
    ppermute x22, waiting for transfers between devices, padded(): before = lax.ppermute(last, axis, up)  43.3 us
    ppermute x22, waiting for transfers between devices, padded(): after = lax.ppermute(initial, axis, down)  17.6 us
    all_gather x2, blocking collectives, gathered_smooth(): lax.all_gather(pack_level(source, initial, diagonal), 'gy', axis=1, tiled...  12.5 us
    ppermute x22, starting transfers between devices, padded(): before = lax.ppermute(last, axis, up)  10.9 us
    dot_general x3, matrix products, prolong_local(): jnp.einsum('abkrj,abkij->abri', picked_lines, blocks, preferred_element_t...  4.93 us
  transfers between devices with their start and end apart: 44, of which 31 were waited for; matrix products, arithmetic and copies ran while one was open for 5% of the time, Pallas kernels for 0%

commit v1 on v0

--- a/solution.py
+++ b/solution.py
@@ -68,7 +68,7 @@
 
 def gathered_smooth(source, initial, diagonal):
     copies = source.shape[2]
-    gathered = lax.all_gather(pack_level(source, initial, diagonal), "gy", axis=1, tiled=True)
+    gathered = jnp.concatenate(lax.all_gather(pack_level(source, initial, diagonal), "gy"), axis=1)
     return chebyshev(
         gathered[:, :, :copies],
         gathered[:, :, copies : 2 * copies],

time: 166 us -> 169 us (1.018)
  waiting for transfers between devices: 60.8 us -> 63.2 us
    ppermute x22, waiting for transfers between devices: 43.3 us -> 45.7 us  [padded(): before = lax.ppermute(last, axis, up)]
    ppermute x22, starting transfers between devices: 10.9 us -> 8.9 us  [padded(): before = lax.ppermute(last, axis, up)]
    ppermute x22, starting transfers between devices: 59.3 us -> 61.3 us  [padded(): after = lax.ppermute(initial, axis, down)]
  transfers between devices with their start and end apart: 44 -> 44, of which waited for: 31 -> 32; matrix products, arithmetic and copies ran while one was open for 5% -> 5% of each run, Pallas kernels for 0% -> 0%
where the time goes in v1:
time: 169 us; the launch traced here: 168 us
  starting transfers between devices  70.2 us (42%)
  waiting for transfers between devices  63.2 us (37%)
  blocking collectives  12 us (7%)
  other arithmetic  9.8 us (6%)
  local copies, waits for them, and re-layouts  6.85 us (4%)
  matrix products  4.93 us (3%)
    ppermute x22, starting transfers between devices, padded(): after = lax.ppermute(initial, axis, down)  61.3 us
    ppermute x22, waiting for transfers between devices, padded(): before = lax.ppermute(last, axis, up)  45.7 us
    ppermute x22, waiting for transfers between devices, padded(): after = lax.ppermute(initial, axis, down)  17.6 us
    all_gather x2, blocking collectives, gathered_smooth(): lax.all_gather(pack_level(source, initial, diagonal), 'gy')  12 us
    ppermute x22, starting transfers between devices, padded(): before = lax.ppermute(last, axis, up)  8.9 us
    dot_general x3, matrix products, prolong_local(): jnp.einsum('abkrj,abkij->abri', picked_lines, blocks, preferred_element_t...  4.93 us
  transfers between devices with their start and end apart: 44, of which 32 were waited for; matrix products, arithmetic and copies ran while one was open for 5% of the time, Pallas kernels for 0%

profile of v1, /device:TPU:0, one launch (start us, length us, event | category | flops | bytes accessed | tf_op | source)
XLA Modules:
  0.0 168.3 jit_solution(4679848375615535220)
XLA Ops:
  1.5 6.2 %all-gather = f32[4,1,33,128]{3,1,2,0:T(1,128)S(1)} all-gather(f32[1,1,33,128]{3,1,2,0:T(1,128)S(1)} %pad_maximum_fusion.83), channel_id=2, replica_groups=mesh['gz'=8,'gy'=4] {'gy'}, dimensions={0}, use_global_device_ids=true | all-gather | bytes 84480 | tf_op jit(solution)/shard_map/all_gather | solution.py:71
  7.7 5.1 %collective-permute-start = (f32[1,4,16,128]{3,1,2,0:T(4,128)S(1)}, f32[1,4,16,128]{3,1,2,0:T(4,128)S(1)}, u32[]{:S(2)}, u32[]{:S(2)}) collective-permute-start(f32[1,4,16,128]{3,1,2,0:T(4,128)S(1)} %slice.670), channel_id=1, source_target_pairs={{4,0},{8,4},{12,8},{16,12},{20,16},{24,20},{28,24},{0,28},{5,1},{9... | collective-permute-start | bytes 98312 | tf_op jit(solution)/shard_map/ppermute | solution.py:20
  17.0 2.4 %collective-permute-done.1 = f32[1,4,16,128]{3,1,2,0:T(4,128)S(1)} collective-permute-done((f32[1,4,16,128]{3,1,2,0:T(4,128)S(1)}, f32[1,4,16,128]{3,1,2,0:T(4,128)S(1)}, u32[]{:S(2)}, u32[]{:S(2)}) %collective-permute-start.1) | collective-permute-done | bytes 32800 | tf_op jit(solution)/shard_map/ppermute | solution.py:19
  19.6 4.7 %collective-permute-start.2 = (f32[1,4,16,128]{3,1,2,0:T(4,128)S(1)}, f32[1,4,16,128]{3,1,2,0:T(4,128)S(1)}, u32[]{:S(2)}, u32[]{:S(2)}) collective-permute-start(f32[1,4,16,128]{3,1,2,0:T(4,128)S(1)} %get-tuple-element.32), channel_id=1, source_target_pairs={{4,0},{8,4},{12,8},{16,12},{20,16},{24,20},{28,24},{0,28},{5,1},{9... | collective-permute-start | bytes 98312 | tf_op jit(solution)/shard_map/ppermute | solution.py:20
  26.4 4.8 %collective-permute-start.4 = (f32[1,4,16,128]{3,1,2,0:T(4,128)S(1)}, f32[1,4,16,128]{3,1,2,0:T(4,128)S(1)}, u32[]{:S(2)}, u32[]{:S(2)}) collective-permute-start(f32[1,4,16,128]{3,1,2,0:T(4,128)S(1)} %get-tuple-element.30), channel_id=1, source_target_pairs={{4,0},{8,4},{12,8},{16,12},{20,16},{24,20},{28,24},{0,28},{5,1},{9... | collective-permute-start | bytes 98312 | tf_op jit(solution)/shard_map/ppermute | solution.py:20
  33.1 4.8 %collective-permute-start.7 = (bf16[1,4,16,128]{3,1,2,0:T(4,128)(2,1)S(1)}, bf16[1,4,16,128]{3,1,2,0:T(4,128)(2,1)S(1)}, u32[]{:S(2)}, u32[]{:S(2)}) collective-permute-start(bf16[1,4,16,128]{3,1,2,0:T(4,128)(2,1)S(1)} %get-tuple-element.28), channel_id=1, source_target_pairs={{4,0},{8,4},{12,8},{16,12},{20,16},{24,20},{28,24},{0,28},{5,1},{9... | collective-permute-start | bytes 49160 | tf_op jit(solution)/shard_map/ppermute | solution.py:20
  39.4 5.0 %collective-permute-done.6 = bf16[1,4,16,128]{3,1,2,0:T(4,128)(2,1)S(1)} collective-permute-done((bf16[1,4,16,128]{3,1,2,0:T(4,128)(2,1)S(1)}, bf16[1,4,16,128]{3,1,2,0:T(4,128)(2,1)S(1)}, u32[]{:S(2)}, u32[]{:S(2)}) %collective-permute-start.6) | collective-permute-done | bytes 16416 | tf_op jit(solution)/shard_map/ppermute | solution.py:19
  47.1 5.8 %all-gather.1 = f32[8,2,33,128]{3,1,2,0:T(2,128)S(1)} all-gather(f32[2,2,33,128]{3,1,2,0:T(2,128)S(1)} %copy.54), channel_id=3, replica_groups=mesh['gz'=8,'gy'=4] {'gy'}, dimensions={0}, use_global_device_ids=true | all-gather | bytes 337920 | tf_op jit(solution)/shard_map/all_gather | solution.py:71
  53.3 2.0 %collective-permute-start.9 = (f32[1,8,16,128]{3,2,1,0:T(8,128)S(1)}, f32[1,8,16,128]{3,2,1,0:T(8,128)S(1)}, u32[]{:S(2)}, u32[]{:S(2)}) collective-permute-start(f32[1,8,16,128]{3,2,1,0:T(8,128)S(1)} %get-tuple-element.59), channel_id=1, source_target_pairs={{0,4},{4,8},{8,12},{12,16},{16,20},{20,24},{24,28},{28,0},{1,5},{5... | collective-permute-start | bytes 196616 | tf_op jit(solution)/shard_map/ppermute | solution.py:19
  55.3 2.3 %collective-permute-done.8 = f32[1,8,16,128]{3,2,1,0:T(8,128)S(1)} collective-permute-done((f32[1,8,16,128]{3,2,1,0:T(8,128)S(1)}, f32[1,8,16,128]{3,2,1,0:T(8,128)S(1)}, u32[]{:S(2)}, u32[]{:S(2)}) %collective-permute-start.8) | collective-permute-done | bytes 65568 | tf_op jit(solution)/shard_map/ppermute | solution.py:20
  57.6 2.8 %collective-permute-done.9 = f32[1,8,16,128]{3,2,1,0:T(8,128)S(1)} collective-permute-done((f32[1,8,16,128]{3,2,1,0:T(8,128)S(1)}, f32[1,8,16,128]{3,2,1,0:T(8,128)S(1)}, u32[]{:S(2)}, u32[]{:S(2)}) %collective-permute-start.9) | collective-permute-done | bytes 65568 | tf_op jit(solution)/shard_map/ppermute | solution.py:19
  62.9 2.2 %collective-permute-done.10 = f32[1,8,16,128]{3,2,1,0:T(8,128)S(1)} collective-permute-done((f32[1,8,16,128]{3,2,1,0:T(8,128)S(1)}, f32[1,8,16,128]{3,2,1,0:T(8,128)S(1)}, u32[]{:S(2)}, u32[]{:S(2)}) %collective-permute-start.10) | collective-permute-done | bytes 65568 | tf_op jit(solution)/shard_map/ppermute | solution.py:20
  65.1 2.9 %collective-permute-done.11 = f32[1,8,16,128]{3,2,1,0:T(8,128)S(1)} collective-permute-done((f32[1,8,16,128]{3,2,1,0:T(8,128)S(1)}, f32[1,8,16,128]{3,2,1,0:T(8,128)S(1)}, u32[]{:S(2)}, u32[]{:S(2)}) %collective-permute-start.11) | collective-permute-done | bytes 65568 | tf_op jit(solution)/shard_map/ppermute | solution.py:19
  68.5 2.0 %collective-permute-start.13 = (f32[1,8,16,128]{3,2,1,0:T(8,128)S(1)}, f32[1,8,16,128]{3,2,1,0:T(8,128)S(1)}, u32[]{:S(2)}, u32[]{:S(2)}) collective-permute-start(f32[1,8,16,128]{3,2,1,0:T(8,128)S(1)} %get-tuple-element.93), channel_id=1, source_target_pairs={{0,4},{4,8},{8,12},{12,16},{16,20},{20,24},{24,28},{28,0},{1,5},{5... | collective-permute-start | bytes 196616 | tf_op jit(solution)/shard_map/ppermute | solution.py:19
  70.5 2.9 %collective-permute-done.12 = f32[1,8,16,128]{3,2,1,0:T(8,128)S(1)} collective-permute-done((f32[1,8,16,128]{3,2,1,0:T(8,128)S(1)}, f32[1,8,16,128]{3,2,1,0:T(8,128)S(1)}, u32[]{:S(2)}, u32[]{:S(2)}) %collective-permute-start.12) | collective-permute-done | bytes 65568 | tf_op jit(solution)/shard_map/ppermute | solution.py:20
  73.5 2.1 %collective-permute-done.13 = f32[1,8,16,128]{3,2,1,0:T(8,128)S(1)} collective-permute-done((f32[1,8,16,128]{3,2,1,0:T(8,128)S(1)}, f32[1,8,16,128]{3,2,1,0:T(8,128)S(1)}, u32[]{:S(2)}, u32[]{:S(2)}) %collective-permute-start.13) | collective-permute-done | bytes 65568 | tf_op jit(solution)/shard_map/ppermute | solution.py:19
  75.8 4.7 %collective-permute-start.15 = (bf16[1,8,16,128]{3,2,1,0:T(8,128)(2,1)S(1)}, bf16[1,8,16,128]{3,2,1,0:T(8,128)(2,1)S(1)}, u32[]{:S(2)}, u32[]{:S(2)}) collective-permute-start(bf16[1,8,16,128]{3,2,1,0:T(8,128)(2,1)S(1)} %get-tuple-element.125), channel_id=1, source_target_pairs={{4,0},{8,4},{12,8},{16,12},{20,16},{24,20},{28,24},{0,28},{5,1},{9... | collective-permute-start | bytes 98312 | tf_op jit(solution)/shard_map/ppermute | solution.py:20
  83.5 4.9 %collective-permute-start.16 = (f32[1,4,16,128]{3,2,1,0:T(8,128)S(1)}, f32[1,4,16,128]{3,2,1,0:T(8,128)S(1)}, u32[]{:S(2)}, u32[]{:S(2)}) collective-permute-start(f32[1,4,16,128]{3,2,1,0:T(8,128)S(1)} %get-tuple-element.87), channel_id=1, source_target_pairs={{4,0},{8,4},{12,8},{16,12},{20,16},{24,20},{28,24},{0,28},{5,1},{9... | collective-permute-start | bytes 98312 | tf_op jit(solution)/shard_map/ppermute | solution.py:20
  92.0 2.3 %collective-permute-done.19 = f32[6,1,16,128]{3,2,1,0:T(8,128)S(1)} collective-permute-done((f32[6,1,16,128]{3,2,1,0:T(8,128)S(1)}, f32[6,1,16,128]{3,2,1,0:T(8,128)S(1)}, u32[]{:S(2)}, u32[]{:S(2)}) %collective-permute-start.19) | collective-permute-done | bytes 49184 | tf_op jit(solution)/shard_map/ppermute | solution.py:19
  94.6 4.8 %collective-permute-start.20 = (f32[1,4,16,128]{3,2,1,0:T(8,128)S(1)}, f32[1,4,16,128]{3,2,1,0:T(8,128)S(1)}, u32[]{:S(2)}, u32[]{:S(2)}) collective-permute-start(f32[1,4,16,128]{3,2,1,0:T(8,128)S(1)} %get-tuple-element.81), channel_id=1, source_target_pairs={{4,0},{8,4},{12,8},{16,12},{20,16},{24,20},{28,24},{0,28},{5,1},{9... | collective-permute-start | bytes 98312 | tf_op jit(solution)/shard_map/ppermute | solution.py:20
  105.1 4.8 %collective-permute-start.24 = (f32[1,4,16,128]{3,2,1,0:T(8,128)S(1)}, f32[1,4,16,128]{3,2,1,0:T(8,128)S(1)}, u32[]{:S(2)}, u32[]{:S(2)}) collective-permute-start(f32[1,4,16,128]{3,2,1,0:T(8,128)S(1)} %get-tuple-element.75), channel_id=1, source_target_pairs={{4,0},{8,4},{12,8},{16,12},{20,16},{24,20},{28,24},{0,28},{5,1},{9... | collective-permute-start | bytes 98312 | tf_op jit(solution)/shard_map/ppermute | solution.py:20
  116.3 4.8 %collective-permute-start.29 = (bf16[1,4,16,128]{3,2,1,0:T(8,128)(2,1)S(1)}, bf16[1,4,16,128]{3,2,1,0:T(8,128)(2,1)S(1)}, u32[]{:S(2)}, u32[]{:S(2)}) collective-permute-start(bf16[1,4,16,128]{3,2,1,0:T(8,128)(2,1)S(1)} %get-tuple-element.123), channel_id=1, source_target_pairs={{4,0},{8,4},{12,8},{16,12},{20,16},{24,20},{28,24},{0,28},{5,1},{9... | collective-permute-start | bytes 49160 | tf_op jit(solution)/shard_map/ppermute | solution.py:20
  126.9 3.4 %fusion = f32[8,8,16,128]{3,2,1,0:T(8,128)S(1)} fusion(f32[8,8,16,128]{3,2,1,0:T(8,128)S(1)} %copy-done.2, bf16[8,8,2,16,128]{4,3,2,1,0:T(8,128)(2,1)S(1)} %bitcast.65, bf16[8,8,2,128,128]{4,3,2,1,0:T(8,128)(2,1)} %param.30), kind=kOutput, calls=%fused_computation.4 | convolution fusion | flops 67239936 | bytes 5767168 | tf_op jit(solution)/shard_map/abkrj,abkij->abri/dot_general | solution.py:91
  130.4 4.8 %collective-permute-start.32 = (f32[1,8,16,128]{3,2,1,0:T(8,128)S(1)}, f32[1,8,16,128]{3,2,1,0:T(8,128)S(1)}, u32[]{:S(2)}, u32[]{:S(2)}) collective-permute-start(f32[1,8,16,128]{3,2,1,0:T(8,128)S(1)} %get-tuple-element.53), channel_id=1, source_target_pairs={{4,0},{8,4},{12,8},{16,12},{20,16},{24,20},{28,24},{0,28},{5,1},{9... | collective-permute-start | bytes 196616 | tf_op jit(solution)/shard_map/ppermute | solution.py:20
  135.4 2.3 %collective-permute-done.33 = f32[1,8,16,128]{3,2,1,0:T(8,128)S(1)} collective-permute-done((f32[1,8,16,128]{3,2,1,0:T(8,128)S(1)}, f32[1,8,16,128]{3,2,1,0:T(8,128)S(1)}, u32[]{:S(2)}, u32[]{:S(2)}) %collective-permute-start.33) | collective-permute-done | bytes 65568 | tf_op jit(solution)/shard_map/ppermute | solution.py:19
  138.8 2.2 %collective-permute-done.34 = f32[10,1,16,128]{3,2,1,0:T(8,128)S(1)} collective-permute-done((f32[10,1,16,128]{3,2,1,0:T(8,128)S(1)}, f32[10,1,16,128]{3,2,1,0:T(8,128)S(1)}, u32[]{:S(2)}, u32[]{:S(2)}) %collective-permute-start.34) | collective-permute-done | bytes 81952 | tf_op jit(solution)/shard_map/ppermute | solution.py:20
  140.9 2.0 %collective-permute-done.35 = f32[10,1,16,128]{3,2,1,0:T(8,128)S(1)} collective-permute-done((f32[10,1,16,128]{3,2,1,0:T(8,128)S(1)}, f32[10,1,16,128]{3,2,1,0:T(8,128)S(1)}, u32[]{:S(2)}, u32[]{:S(2)}) %collective-permute-start.35) | collective-permute-done | bytes 81952 | tf_op jit(solution)/shard_map/ppermute | solution.py:19
  143.4 5.0 %collective-permute-start.36 = (f32[1,8,16,128]{3,2,1,0:T(8,128)S(1)}, f32[1,8,16,128]{3,2,1,0:T(8,128)S(1)}, u32[]{:S(2)}, u32[]{:S(2)}) collective-permute-start(f32[1,8,16,128]{3,2,1,0:T(8,128)S(1)} %get-tuple-element.47), channel_id=1, source_target_pairs={{4,0},{8,4},{12,8},{16,12},{20,16},{24,20},{28,24},{0,28},{5,1},{9... | collective-permute-start | bytes 196616 | tf_op jit(solution)/shard_map/ppermute | solution.py:20
  148.7 2.0 %collective-permute-done.37 = f32[1,8,16,128]{3,2,1,0:T(8,128)S(1)} collective-permute-done((f32[1,8,16,128]{3,2,1,0:T(8,128)S(1)}, f32[1,8,16,128]{3,2,1,0:T(8,128)S(1)}, u32[]{:S(2)}, u32[]{:S(2)}) %collective-permute-start.37) | collective-permute-done | bytes 65568 | tf_op jit(solution)/shard_map/ppermute | solution.py:19
  155.5 4.8 %collective-permute-start.40 = (f32[1,8,16,128]{3,2,1,0:T(8,128)S(1)}, f32[1,8,16,128]{3,2,1,0:T(8,128)S(1)}, u32[]{:S(2)}, u32[]{:S(2)}) collective-permute-start(f32[1,8,16,128]{3,2,1,0:T(8,128)S(1)} %get-tuple-element.45), channel_id=1, source_target_pairs={{4,0},{8,4},{12,8},{16,12},{20,16},{24,20},{28,24},{0,28},{5,1},{9... | collective-permute-start | bytes 196616 | tf_op jit(solution)/shard_map/ppermute | solution.py:20
  160.6 2.0 %collective-permute-done.41 = f32[1,8,16,128]{3,2,1,0:T(8,128)S(1)} collective-permute-done((f32[1,8,16,128]{3,2,1,0:T(8,128)S(1)}, f32[1,8,16,128]{3,2,1,0:T(8,128)S(1)}, u32[]{:S(2)}, u32[]{:S(2)}) %collective-permute-start.41) | collective-permute-done | bytes 65568 | tf_op jit(solution)/shard_map/ppermute | solution.py:19
  164.9 2.1 %collective-permute-done.43 = f32[10,1,16,128]{3,2,1,0:T(8,128)S(1)} collective-permute-done((f32[10,1,16,128]{3,2,1,0:T(8,128)S(1)}, f32[10,1,16,128]{3,2,1,0:T(8,128)S(1)}, u32[]{:S(2)}, u32[]{:S(2)}) %collective-permute-start.43) | collective-permute-done | bytes 81952 | tf_op jit(solution)/shard_map/ppermute | solution.py:19
  (172 shorter events, 52.1 us)
Async XLA Ops:
  7.7 9.3 %collective-permute-start = (f32[1,4,16,128]{3,1,2,0:T(4,128)S(1)}, f32[1,4,16,128]{3,1,2,0:T(4,128)S(1)}, u32[]{:S(2)}, u32[]{:S(2)}) collective-permute-start(f32[1,4,16,128]{3,1,2,0:T(4,128)S(1)} %slice.670), channel_id=1, source_target_pairs={{4,0},{8,4},{12,8},{16,12},{20,16},{24,20},{28,24},{0,28},{5,1},{9... | collective-permute-start | bytes 98312 | tf_op jit(solution)/shard_map/ppermute | solution.py:20
  12.8 6.6 %collective-permute-start.1 = (f32[1,4,16,128]{3,1,2,0:T(4,128)S(1)}, f32[1,4,16,128]{3,1,2,0:T(4,128)S(1)}, u32[]{:S(2)}, u32[]{:S(2)}) collective-permute-start(f32[1,4,16,128]{3,1,2,0:T(4,128)S(1)} %slice.670), channel_id=1, source_target_pairs={{0,4},{4,8},{8,12},{12,16},{16,20},{20,24},{24,28},{28,0},{1,5},{5... | collective-permute-start | bytes 98312 | tf_op jit(solution)/shard_map/ppermute | solution.py:19
  19.5 6.7 %collective-permute-start.3 = (f32[1,4,16,128]{3,1,2,0:T(4,128)S(1)}, f32[1,4,16,128]{3,1,2,0:T(4,128)S(1)}, u32[]{:S(2)}, u32[]{:S(2)}) collective-permute-start(f32[1,4,16,128]{3,1,2,0:T(4,128)S(1)} %get-tuple-element.32), channel_id=1, source_target_pairs={{0,4},{4,8},{8,12},{12,16},{16,20},{20,24},{24,28},{28,0},{1,5},{5... | collective-permute-start | bytes 98312 | tf_op jit(solution)/shard_map/ppermute | solution.py:19
  19.6 6.6 %collective-permute-start.2 = (f32[1,4,16,128]{3,1,2,0:T(4,128)S(1)}, f32[1,4,16,128]{3,1,2,0:T(4,128)S(1)}, u32[]{:S(2)}, u32[]{:S(2)}) collective-permute-start(f32[1,4,16,128]{3,1,2,0:T(4,128)S(1)} %get-tuple-element.32), channel_id=1, source_target_pairs={{4,0},{8,4},{12,8},{16,12},{20,16},{24,20},{28,24},{0,28},{5,1},{9... | collective-permute-start | bytes 98312 | tf_op jit(solution)/shard_map/ppermute | solution.py:20
  26.3 6.7 %collective-permute-start.5 = (f32[1,4,16,128]{3,1,2,0:T(4,128)S(1)}, f32[1,4,16,128]{3,1,2,0:T(4,128)S(1)}, u32[]{:S(2)}, u32[]{:S(2)}) collective-permute-start(f32[1,4,16,128]{3,1,2,0:T(4,128)S(1)} %get-tuple-element.30), channel_id=1, source_target_pairs={{0,4},{4,8},{8,12},{12,16},{16,20},{20,24},{24,28},{28,0},{1,5},{5... | collective-permute-start | bytes 98312 | tf_op jit(solution)/shard_map/ppermute | solution.py:19
  26.4 6.6 %collective-permute-start.4 = (f32[1,4,16,128]{3,1,2,0:T(4,128)S(1)}, f32[1,4,16,128]{3,1,2,0:T(4,128)S(1)}, u32[]{:S(2)}, u32[]{:S(2)}) collective-permute-start(f32[1,4,16,128]{3,1,2,0:T(4,128)S(1)} %get-tuple-element.30), channel_id=1, source_target_pairs={{4,0},{8,4},{12,8},{16,12},{20,16},{24,20},{28,24},{0,28},{5,1},{9... | collective-permute-start | bytes 98312 | tf_op jit(solution)/shard_map/ppermute | solution.py:20
  33.1 6.3 %collective-permute-start.7 = (bf16[1,4,16,128]{3,1,2,0:T(4,128)(2,1)S(1)}, bf16[1,4,16,128]{3,1,2,0:T(4,128)(2,1)S(1)}, u32[]{:S(2)}, u32[]{:S(2)}) collective-permute-start(bf16[1,4,16,128]{3,1,2,0:T(4,128)(2,1)S(1)} %get-tuple-element.28), channel_id=1, source_target_pairs={{4,0},{8,4},{12,8},{16,12},{20,16},{24,20},{28,24},{0,28},{5,1},{9... | collective-permute-start | bytes 49160 | tf_op jit(solution)/shard_map/ppermute | solution.py:20
  37.9 6.4 %collective-permute-start.6 = (bf16[1,4,16,128]{3,1,2,0:T(4,128)(2,1)S(1)}, bf16[1,4,16,128]{3,1,2,0:T(4,128)(2,1)S(1)}, u32[]{:S(2)}, u32[]{:S(2)}) collective-permute-start(bf16[1,4,16,128]{3,1,2,0:T(4,128)(2,1)S(1)} %get-tuple-element.28), channel_id=1, source_target_pairs={{0,4},{4,8},{8,12},{12,16},{16,20},{20,24},{24,28},{28,0},{1,5},{5... | collective-permute-start | bytes 49160 | tf_op jit(solution)/shard_map/ppermute | solution.py:19
  53.2 4.4 %collective-permute-start.8 = (f32[1,8,16,128]{3,2,1,0:T(8,128)S(1)}, f32[1,8,16,128]{3,2,1,0:T(8,128)S(1)}, u32[]{:S(2)}, u32[]{:S(2)}) collective-permute-start(f32[1,8,16,128]{3,2,1,0:T(8,128)S(1)} %get-tuple-element.58), channel_id=1, source_target_pairs={{4,0},{8,4},{12,8},{16,12},{20,16},{24,20},{28,24},{0,28},{5,1},{9... | collective-permute-start | bytes 196616 | tf_op jit(solution)/shard_map/ppermute | solution.py:20
  53.3 7.1 %collective-permute-start.9 = (f32[1,8,16,128]{3,2,1,0:T(8,128)S(1)}, f32[1,8,16,128]{3,2,1,0:T(8,128)S(1)}, u32[]{:S(2)}, u32[]{:S(2)}) collective-permute-start(f32[1,8,16,128]{3,2,1,0:T(8,128)S(1)} %get-tuple-element.59), channel_id=1, source_target_pairs={{0,4},{4,8},{8,12},{12,16},{16,20},{20,24},{24,28},{28,0},{1,5},{5... | collective-permute-start | bytes 196616 | tf_op jit(solution)/shard_map/ppermute | solution.py:19
  60.8 4.3 %collective-permute-start.10 = (f32[1,8,16,128]{3,2,1,0:T(8,128)S(1)}, f32[1,8,16,128]{3,2,1,0:T(8,128)S(1)}, u32[]{:S(2)}, u32[]{:S(2)}) collective-permute-start(f32[1,8,16,128]{3,2,1,0:T(8,128)S(1)} %get-tuple-element.102), channel_id=1, source_target_pairs={{4,0},{8,4},{12,8},{16,12},{20,16},{24,20},{28,24},{0,28},{5,1},{9... | collective-permute-start | bytes 196616 | tf_op jit(solution)/shard_map/ppermute | solution.py:20
  61.1 7.0 %collective-permute-start.11 = (f32[1,8,16,128]{3,2,1,0:T(8,128)S(1)}, f32[1,8,16,128]{3,2,1,0:T(8,128)S(1)}, u32[]{:S(2)}, u32[]{:S(2)}) collective-permute-start(f32[1,8,16,128]{3,2,1,0:T(8,128)S(1)} %get-tuple-element.103), channel_id=1, source_target_pairs={{0,4},{4,8},{8,12},{12,16},{16,20},{20,24},{24,28},{28,0},{1,5},{5... | collective-permute-start | bytes 196616 | tf_op jit(solution)/shard_map/ppermute | solution.py:19
  68.4 5.0 %collective-permute-start.12 = (f32[1,8,16,128]{3,2,1,0:T(8,128)S(1)}, f32[1,8,16,128]{3,2,1,0:T(8,128)S(1)}, u32[]{:S(2)}, u32[]{:S(2)}) collective-permute-start(f32[1,8,16,128]{3,2,1,0:T(8,128)S(1)} %get-tuple-element.92), channel_id=1, source_target_pairs={{4,0},{8,4},{12,8},{16,12},{20,16},{24,20},{28,24},{0,28},{5,1},{9... | collective-permute-start | bytes 196616 | tf_op jit(solution)/shard_map/ppermute | solution.py:20
  68.5 7.0 %collective-permute-start.13 = (f32[1,8,16,128]{3,2,1,0:T(8,128)S(1)}, f32[1,8,16,128]{3,2,1,0:T(8,128)S(1)}, u32[]{:S(2)}, u32[]{:S(2)}) collective-permute-start(f32[1,8,16,128]{3,2,1,0:T(8,128)S(1)} %get-tuple-element.93), channel_id=1, source_target_pairs={{0,4},{4,8},{8,12},{12,16},{16,20},{20,24},{24,28},{28,0},{1,5},{5... | collective-permute-start | bytes 196616 | tf_op jit(solution)/shard_map/ppermute | solution.py:19
  75.7 6.7 %collective-permute-start.14 = (bf16[1,8,16,128]{3,2,1,0:T(8,128)(2,1)S(1)}, bf16[1,8,16,128]{3,2,1,0:T(8,128)(2,1)S(1)}, u32[]{:S(2)}, u32[]{:S(2)}) collective-permute-start(bf16[1,8,16,128]{3,2,1,0:T(8,128)(2,1)S(1)} %get-tuple-element.124), channel_id=1, source_target_pairs={{0,4},{4,8},{8,12},{12,16},{16,20},{20,24},{24,28},{28,0},{1,5},{5... | collective-permute-start | bytes 98312 | tf_op jit(solution)/shard_map/ppermute | solution.py:19
  75.8 6.6 %collective-permute-start.15 = (bf16[1,8,16,128]{3,2,1,0:T(8,128)(2,1)S(1)}, bf16[1,8,16,128]{3,2,1,0:T(8,128)(2,1)S(1)}, u32[]{:S(2)}, u32[]{:S(2)}) collective-permute-start(bf16[1,8,16,128]{3,2,1,0:T(8,128)(2,1)S(1)} %get-tuple-element.125), channel_id=1, source_target_pairs={{4,0},{8,4},{12,8},{16,12},{20,16},{24,20},{28,24},{0,28},{5,1},{9... | collective-permute-start | bytes 98312 | tf_op jit(solution)/shard_map/ppermute | solution.py:20
  83.4 6.8 %collective-permute-start.17 = (f32[1,4,16,128]{3,2,1,0:T(8,128)S(1)}, f32[1,4,16,128]{3,2,1,0:T(8,128)S(1)}, u32[]{:S(2)}, u32[]{:S(2)}) collective-permute-start(f32[1,4,16,128]{3,2,1,0:T(8,128)S(1)} %get-tuple-element.86), channel_id=1, source_target_pairs={{0,4},{4,8},{8,12},{12,16},{16,20},{20,24},{24,28},{28,0},{1,5},{5... | collective-permute-start | bytes 98312 | tf_op jit(solution)/shard_map/ppermute | solution.py:19
  83.5 6.7 %collective-permute-start.16 = (f32[1,4,16,128]{3,2,1,0:T(8,128)S(1)}, f32[1,4,16,128]{3,2,1,0:T(8,128)S(1)}, u32[]{:S(2)}, u32[]{:S(2)}) collective-permute-start(f32[1,4,16,128]{3,2,1,0:T(8,128)S(1)} %get-tuple-element.87), channel_id=1, source_target_pairs={{4,0},{8,4},{12,8},{16,12},{20,16},{24,20},{28,24},{0,28},{5,1},{9... | collective-permute-start | bytes 98312 | tf_op jit(solution)/shard_map/ppermute | solution.py:20
  94.5 6.7 %collective-permute-start.21 = (f32[1,4,16,128]{3,2,1,0:T(8,128)S(1)}, f32[1,4,16,128]{3,2,1,0:T(8,128)S(1)}, u32[]{:S(2)}, u32[]{:S(2)}) collective-permute-start(f32[1,4,16,128]{3,2,1,0:T(8,128)S(1)} %get-tuple-element.80), channel_id=1, source_target_pairs={{0,4},{4,8},{8,12},{12,16},{16,20},{20,24},{24,28},{28,0},{1,5},{5... | collective-permute-start | bytes 98312 | tf_op jit(solution)/shard_map/ppermute | solution.py:19
  94.6 6.7 %collective-permute-start.20 = (f32[1,4,16,128]{3,2,1,0:T(8,128)S(1)}, f32[1,4,16,128]{3,2,1,0:T(8,128)S(1)}, u32[]{:S(2)}, u32[]{:S(2)}) collective-permute-start(f32[1,4,16,128]{3,2,1,0:T(8,128)S(1)} %get-tuple-element.81), channel_id=1, source_target_pairs={{4,0},{8,4},{12,8},{16,12},{20,16},{24,20},{28,24},{0,28},{5,1},{9... | collective-permute-start | bytes 98312 | tf_op jit(solution)/shard_map/ppermute | solution.py:20
  105.1 6.7 %collective-permute-start.25 = (f32[1,4,16,128]{3,2,1,0:T(8,128)S(1)}, f32[1,4,16,128]{3,2,1,0:T(8,128)S(1)}, u32[]{:S(2)}, u32[]{:S(2)}) collective-permute-start(f32[1,4,16,128]{3,2,1,0:T(8,128)S(1)} %get-tuple-element.74), channel_id=1, source_target_pairs={{0,4},{4,8},{8,12},{12,16},{16,20},{20,24},{24,28},{28,0},{1,5},{5... | collective-permute-start | bytes 98312 | tf_op jit(solution)/shard_map/ppermute | solution.py:19
  105.1 6.7 %collective-permute-start.24 = (f32[1,4,16,128]{3,2,1,0:T(8,128)S(1)}, f32[1,4,16,128]{3,2,1,0:T(8,128)S(1)}, u32[]{:S(2)}, u32[]{:S(2)}) collective-permute-start(f32[1,4,16,128]{3,2,1,0:T(8,128)S(1)} %get-tuple-element.75), channel_id=1, source_target_pairs={{4,0},{8,4},{12,8},{16,12},{20,16},{24,20},{28,24},{0,28},{5,1},{9... | collective-permute-start | bytes 98312 | tf_op jit(solution)/shard_map/ppermute | solution.py:20
  116.3 6.5 %collective-permute-start.28 = (bf16[1,4,16,128]{3,2,1,0:T(8,128)(2,1)S(1)}, bf16[1,4,16,128]{3,2,1,0:T(8,128)(2,1)S(1)}, u32[]{:S(2)}, u32[]{:S(2)}) collective-permute-start(bf16[1,4,16,128]{3,2,1,0:T(8,128)(2,1)S(1)} %get-tuple-element.122), channel_id=1, source_target_pairs={{0,4},{4,8},{8,12},{12,16},{16,20},{20,24},{24,28},{28,0},{1,5},{5... | collective-permute-start | bytes 49160 | tf_op jit(solution)/shard_map/ppermute | solution.py:19
  116.3 6.5 %collective-permute-start.29 = (bf16[1,4,16,128]{3,2,1,0:T(8,128)(2,1)S(1)}, bf16[1,4,16,128]{3,2,1,0:T(8,128)(2,1)S(1)}, u32[]{:S(2)}, u32[]{:S(2)}) collective-permute-start(bf16[1,4,16,128]{3,2,1,0:T(8,128)(2,1)S(1)} %get-tuple-element.123), channel_id=1, source_target_pairs={{4,0},{8,4},{12,8},{16,12},{20,16},{24,20},{28,24},{0,28},{5,1},{9... | collective-permute-start | bytes 49160 | tf_op jit(solution)/shard_map/ppermute | solution.py:20
  130.4 7.3 %collective-permute-start.33 = (f32[1,8,16,128]{3,2,1,0:T(8,128)S(1)}, f32[1,8,16,128]{3,2,1,0:T(8,128)S(1)}, u32[]{:S(2)}, u32[]{:S(2)}) collective-permute-start(f32[1,8,16,128]{3,2,1,0:T(8,128)S(1)} %get-tuple-element.52), channel_id=1, source_target_pairs={{0,4},{4,8},{8,12},{12,16},{16,20},{20,24},{24,28},{28,0},{1,5},{5... | collective-permute-start | bytes 196616 | tf_op jit(solution)/shard_map/ppermute | solution.py:19
  130.4 7.3 %collective-permute-start.32 = (f32[1,8,16,128]{3,2,1,0:T(8,128)S(1)}, f32[1,8,16,128]{3,2,1,0:T(8,128)S(1)}, u32[]{:S(2)}, u32[]{:S(2)}) collective-permute-start(f32[1,8,16,128]{3,2,1,0:T(8,128)S(1)} %get-tuple-element.53), channel_id=1, source_target_pairs={{4,0},{8,4},{12,8},{16,12},{20,16},{24,20},{28,24},{0,28},{5,1},{9... | collective-permute-start | bytes 196616 | tf_op jit(solution)/shard_map/ppermute | solution.py:20
  138.6 4.3 %collective-permute-start.35 = (f32[10,1,16,128]{3,2,1,0:T(8,128)S(1)}, f32[10,1,16,128]{3,2,1,0:T(8,128)S(1)}, u32[]{:S(2)}, u32[]{:S(2)}) collective-permute-start(f32[10,1,16,128]{3,2,1,0:T(8,128)S(1)} %get-tuple-element.39), channel_id=1, source_target_pairs={{0,1},{1,2},{2,3},{3,0},{4,5},{5,6},{6,7},{7,4},{8,9},{9,10},{10,1... | collective-permute-start | bytes 245768 | tf_op jit(solution)/shard_map/ppermute | solution.py:19
  143.4 7.3 %collective-permute-start.37 = (f32[1,8,16,128]{3,2,1,0:T(8,128)S(1)}, f32[1,8,16,128]{3,2,1,0:T(8,128)S(1)}, u32[]{:S(2)}, u32[]{:S(2)}) collective-permute-start(f32[1,8,16,128]{3,2,1,0:T(8,128)S(1)} %get-tuple-element.46), channel_id=1, source_target_pairs={{0,4},{4,8},{8,12},{12,16},{16,20},{20,24},{24,28},{28,0},{1,5},{5... | collective-permute-start | bytes 196616 | tf_op jit(solution)/shard_map/ppermute | solution.py:19
  143.4 7.2 %collective-permute-start.36 = (f32[1,8,16,128]{3,2,1,0:T(8,128)S(1)}, f32[1,8,16,128]{3,2,1,0:T(8,128)S(1)}, u32[]{:S(2)}, u32[]{:S(2)}) collective-permute-start(f32[1,8,16,128]{3,2,1,0:T(8,128)S(1)} %get-tuple-element.47), channel_id=1, source_target_pairs={{4,0},{8,4},{12,8},{16,12},{20,16},{24,20},{28,24},{0,28},{5,1},{9... | collective-permute-start | bytes 196616 | tf_op jit(solution)/shard_map/ppermute | solution.py:20
  155.5 7.1 %collective-permute-start.41 = (f32[1,8,16,128]{3,2,1,0:T(8,128)S(1)}, f32[1,8,16,128]{3,2,1,0:T(8,128)S(1)}, u32[]{:S(2)}, u32[]{:S(2)}) collective-permute-start(f32[1,8,16,128]{3,2,1,0:T(8,128)S(1)} %get-tuple-element.44), channel_id=1, source_target_pairs={{0,4},{4,8},{8,12},{12,16},{16,20},{20,24},{24,28},{28,0},{1,5},{5... | collective-permute-start | bytes 196616 | tf_op jit(solution)/shard_map/ppermute | solution.py:19
  155.5 7.0 %collective-permute-start.40 = (f32[1,8,16,128]{3,2,1,0:T(8,128)S(1)}, f32[1,8,16,128]{3,2,1,0:T(8,128)S(1)}, u32[]{:S(2)}, u32[]{:S(2)}) collective-permute-start(f32[1,8,16,128]{3,2,1,0:T(8,128)S(1)} %get-tuple-element.45), channel_id=1, source_target_pairs={{4,0},{8,4},{12,8},{16,12},{20,16},{24,20},{28,24},{0,28},{5,1},{9... | collective-permute-start | bytes 196616 | tf_op jit(solution)/shard_map/ppermute | solution.py:20
  162.6 4.4 %collective-permute-start.43 = (f32[10,1,16,128]{3,2,1,0:T(8,128)S(1)}, f32[10,1,16,128]{3,2,1,0:T(8,128)S(1)}, u32[]{:S(2)}, u32[]{:S(2)}) collective-permute-start(f32[10,1,16,128]{3,2,1,0:T(8,128)S(1)} %get-tuple-element.35), channel_id=1, source_target_pairs={{0,1},{1,2},{2,3},{3,0},{4,5},{5,6},{6,7},{7,4},{8,9},{9,10},{10,1... | collective-permute-start | bytes 245768 | tf_op jit(solution)/shard_map/ppermute | solution.py:19
  (17 other events, 215.3 us)
